TPU v7x, 32 devices: a whole 2x2x4 slice. The times are simulated.
32 devices in a mesh: group: 8 (over z, x), peer: 4 (over y, core).
Axes of the slice: x: 2, y: 2, z: 4, core: 2. Of those that a mesh axis runs over, the one named last changes fastest.
Arguments:
- features: bfloat16 [12288, 1024], P(('group', 'peer')), may hold values from -6 to 6
- task_mask: int32 [12288], P(('group', 'peer')), may hold values from 0 to 65535, as said below
- tower_in: bfloat16 [16, 2048, 1024], P('peer', 'group'), may hold values from -0.1875 to 0.1875
- tower_bias: bfloat16 [16, 2048], P('peer', 'group'), may hold values from -5 to 5
- tower_head: bfloat16 [16, 2048], P('peer', 'group'), may hold values from -0.125 to 0.125
- head_bias: float32 [16], P('peer'), may hold values from -4 to 4
Outputs:
- predictions: float32 [12288, 16], P(('group', 'peer'))
Inputs may be any that keep to these rules, and one draw needn't show every extreme that they name: `task_mask`: only bits 0 to 15 are used. Among the 384 samples of one device (aligned blocks of 384), at most 176 have any one bit set; in every run of 4 blocks that one group holds, some task's bit is set exactly 176 times in each block.
All inputs are finite; a program needn't handle non-finite values.
Results may differ from a plain program's by a relative error of at most 0.0003.
Values may be sent and summed in bfloat16 or wider, within the bound.
A program may use at most 128 MiB of HBM per device.

v0:
```python
import jax
import jax.numpy as jnp
from jax import lax
from jax.sharding import PartitionSpec as P

CAP = 176


def shards(features, task_mask, tower_in, tower_bias, tower_head, head_bias):
    peers = lax.axis_size("peer")
    local_tasks = tower_in.shape[0]
    all_tasks = local_tasks * peers
    task_ids = jnp.arange(all_tasks, dtype=jnp.int32)
    slot_indices = jnp.arange(CAP, dtype=jnp.int32)
    task_bits = task_mask[:, None] >> task_ids[None, :] & 1
    inclusive = jnp.cumsum(task_bits, axis=0)
    slot_rank = inclusive - task_bits
    task_selector = (slot_rank.T[:, None, :] == slot_indices[None, :, None]) & (
        task_bits.T[:, None, :] == 1
    )
    outgoing = jnp.einsum(
        "yra,az->yrz",
        task_selector.astype(jnp.bfloat16),
        features,
        preferred_element_type=jnp.float32,
    ).astype(jnp.bfloat16)
    outgoing = outgoing.reshape(peers, local_tasks, CAP, features.shape[1])
    arrived = lax.all_to_all(outgoing, "peer", split_axis=0, concat_axis=0, tiled=True)
    weight = lax.all_gather(tower_in, "group", axis=1, tiled=True)
    hidden_unit_bias = lax.all_gather(tower_bias, "group", axis=1, tiled=True)
    head_row = lax.all_gather(tower_head, "group", axis=1, tiled=True)
    preact = jnp.einsum("sjcd,jhd->sjch", arrived, weight, preferred_element_type=jnp.float32)
    hidden = jnp.maximum(preact + hidden_unit_bias.astype(jnp.float32)[None, :, None, :], 0.0)
    logits = jnp.einsum(
        "sjch,jh->sjc", hidden, head_row.astype(jnp.float32), precision=lax.Precision.HIGHEST
    )
    logits = logits + head_bias[None, :, None]
    returned_output = lax.all_to_all(
        logits, "peer", split_axis=0, concat_axis=0, tiled=True
    ).reshape(all_tasks, CAP)
    task_selector = (slot_rank.T[:, None, :] == slot_indices[None, :, None]) & (
        task_bits.T[:, None, :] == 1
    )
    return jnp.einsum(
        "ivf,iv->fi",
        task_selector.astype(jnp.float32),
        returned_output,
        precision=lax.Precision.HIGHEST,
    )


def solution(mesh):
    placed = (
        P(("group", "peer"), None),
        P(("group", "peer")),
        P("peer", "group", None),
        P("peer", "group"),
        P("peer", "group"),
        P("peer"),
    )
    return jax.shard_map(
        shards, mesh=mesh, in_specs=placed, out_specs=P(("group", "peer"), None), check_vma=False
    )
```

profile of v0, /device:TPU:0, one launch (start us, length us, event | category | flops | bytes accessed | tf_op | source)
XLA Modules:
  0.0 291.0 jit_solution(16052179998820379908)
XLA Ops:
  6.5 0.0 copy-start
  6.5 0.0 all-gather.2.cloned.1.call-start
  6.5 0.7 all-gather.2.cloned.1.call-update
  7.3 0.7 shift-right-arithmetic_and_fusion.1
  7.9 0.9 reduce-window.6
  8.8 0.2 slice_reduce_fusion
  9.1 0.7 fusion.23
  9.8 0.8 bitcast_subtract_fusion
  10.5 0.0 copy-done
  10.5 4.9 %fusion.14 = bf16[16,176,1024]{2,1,0:T(8,128)(2,1)} fusion(s32[16,384]{1,0:T(8,128)S(1)} %bitcast_subtract_fusion, pred[16,384]{1,0:T(8,128)(4,1)S(1)} %fusion.23, bf16[384,1024]{1,0:T(8,128)(2,1)S(1)} %copy-done), kind=kOutput, calls=%fused_computation.13 | convolution fusion | flops 2219638784 | bytes 6584320 | tf_op jit(solution)/shard_map/yra,az->yrz/dot_general | solution.py:21
  15.4 0.0 copy-start.1
  15.4 0.0 copy-start.2
  15.4 5.3 %all-to-all-start = ((bf16[4,4,176,1024]{3,2,1,0:T(8,128)(2,1)}), bf16[4,4,176,1024]{3,2,1,0:T(8,128)(2,1)}, u32[]{:S(2)}, u32[]{:S(2)}) async-start(bf16[4,4,176,1024]{3,2,1,0:T(8,128)(2,1)} %bitcast.32), calls=%async_computation | async-start | bytes 11534336 | tf_op jit(solution)/shard_map/all_to_all | solution.py:28
  20.7 0.0 copy-done.1
  20.7 29.4 %all_gather.10 = bf16[4,2048]{1,0:T(4,128)(2,1)S(1)} all-gather(bf16[4,256]{1,0:T(4,128)(2,1)S(1)} %copy-done.1), channel_id=1, replica_groups=mesh['group'=8,'peer'=4] {'group'}, dimensions={1}, use_global_device_ids=true | all-gather | bytes 18432 | tf_op jit(solution)/shard_map/all_gather | solution.py:30
  50.2 0.0 copy-done.2
  50.2 27.3 %all_gather.11 = bf16[4,2048]{1,0:T(4,128)(2,1)S(1)} all-gather(bf16[4,256]{1,0:T(4,128)(2,1)S(1)} %copy-done.2), channel_id=1, replica_groups=mesh['group'=8,'peer'=4] {'group'}, dimensions={1}, use_global_device_ids=true | all-gather | bytes 18432 | tf_op jit(solution)/shard_map/all_gather | solution.py:31
  77.5 9.2 %all-to-all-done = bf16[4,4,176,1024]{3,2,1,0:T(8,128)(2,1)} async-done(((bf16[4,4,176,1024]{3,2,1,0:T(8,128)(2,1)}), bf16[4,4,176,1024]{3,2,1,0:T(8,128)(2,1)}, u32[]{:S(2)}, u32[]{:S(2)}) %all-to-all-start) | async-done | bytes 5767200 | tf_op jit(solution)/shard_map/all_to_all | solution.py:28
  86.7 153.3 %all-gather.2.cloned.1.call-done = bf16[4,2048,1024]{2,1,0:T(8,128)(2,1)} async-done(((bf16[4,256,1024]{2,1,0:T(8,128)(2,1)}), bf16[4,2048,1024]{2,1,0:T(8,128)(2,1)}) %all-gather.2.cloned.1.call-update) | async-done | bytes 16777232 | tf_op jit(solution)/shard_map/all_gather | solution.py:29
  240.0 20.6 %fusion.4 = f32[4,4,176,2048]{3,2,1,0:T(8,128)} fusion(bf16[4,2048,1024]{2,1,0:T(8,128)(2,1)} %all-gather.2.cloned.1.call-done, bf16[4,4,176,1024]{3,2,1,0:T(8,128)(2,1)} %all-to-all-done), kind=kOutput, calls=%fused_computation.4 | convolution fusion | flops 11811160064 | bytes 45613056 | tf_op jit(solution)/shard_map/sjcd,jhd->sjch/dot_general | solution.py:32
  260.6 0.0 copy-start.3
  260.6 14.7 %fusion = f32[4,1,4,176]{3,1,2,0:T(1,128)S(1)} fusion(f32[4,4,176,2048]{3,2,1,0:T(8,128)} %fusion.4, f32[4,2048]{1,0:T(4,128)S(1)} %convert_element_type.10, bf16[4,2048,1,1]{1,0,2,3:T(4,128)(2,1)S(1)} %bitcast.33), kind=kOutput, calls=%fused_computation | convolution fusion | flops 80740352 | bytes 23129088 | tf_op jit(solution)/shard_map/sjch,jh->sjc/dot_general | solution.py:34
  275.3 0.0 copy-done.3
  275.3 0.1 fusion.24
  275.4 6.4 %all_to_all.10 = f32[4,4,176]{2,1,0:T(4,128)S(1)} all-to-all(f32[4,4,176]{2,1,0:T(4,128)S(1)} %fusion.24), channel_id=1, replica_groups=mesh['group'=8,'peer'=4] {'peer'}, dimensions={0} | all-to-all | bytes 22528 | tf_op jit(solution)/shard_map/all_to_all | solution.py:38
  281.8 1.8 fusion.10
  283.6 0.6 copy.22
  (3 shorter events, 0.1 us)
Async XLA Ops:
  6.5 4.0 %copy-start = (bf16[384,1024]{1,0:T(8,128)(2,1)S(1)}, bf16[384,1024]{1,0:T(8,128)(2,1)}, u32[]{:S(2)}) copy-start(bf16[384,1024]{1,0:T(8,128)(2,1)} %param.6) | copy-start | bytes 2359300
  6.5 233.5 %all-gather.2.cloned.1.call-start = ((), (), s32[]{:S(2)}) async-start(), calls=%async_computation.2 | async-start | bytes 18874368 | tf_op jit(solution)/shard_map/all_gather | solution.py:29
  15.4 5.3 %copy-start.1 = (bf16[4,256]{1,0:T(4,128)(2,1)S(1)}, bf16[4,256]{1,0:T(4,128)(2,1)}, u32[]{:S(2)}) copy-start(bf16[4,256]{1,0:T(4,128)(2,1)} %param.9) | copy-start | bytes 6148
  15.4 34.7 %copy-start.2 = (bf16[4,256]{1,0:T(4,128)(2,1)S(1)}, bf16[4,256]{1,0:T(4,128)(2,1)}, u32[]{:S(2)}) copy-start(bf16[4,256]{1,0:T(4,128)(2,1)} %param.10) | copy-start | bytes 6148
  15.4 71.2 %all-to-all-start = ((bf16[4,4,176,1024]{3,2,1,0:T(8,128)(2,1)}), bf16[4,4,176,1024]{3,2,1,0:T(8,128)(2,1)}, u32[]{:S(2)}, u32[]{:S(2)}) async-start(bf16[4,4,176,1024]{3,2,1,0:T(8,128)(2,1)} %bitcast.32), calls=%async_computation | async-start | bytes 11534336 | tf_op jit(solution)/shard_map/all_to_all | solution.py:28
  260.6 14.7 %copy-start.3 = (f32[4]{0:T(128)S(1)}, f32[4]{0:T(128)}, u32[]{:S(2)}) copy-start(f32[4]{0:T(128)} %param.11) | copy-start | bytes 52
Sparse Core Ops, SparseCore 0:
  9.5 230.4 all-gather.1
where the time goes:
time: 291 us
  waiting for transfers between devices  163 us (56%)
  blocking collectives  63.1 us (22%)
  matrix products  42 us (14%)
  between operations  13.4 us (5%)
  starting transfers between devices  5.26 us (2%)
  other arithmetic  3.12 us (1%)
    all_gather x1, waiting for transfers between devices, shards(): weight = lax.all_gather(tower_in, 'group', axis=1, tiled=True)  153 us
    all_gather x1, blocking collectives, shards(): hidden_unit_bias = lax.all_gather(tower_bias, 'group', axis=1, tiled=True)  29.4 us
    all_gather x1, blocking collectives, shards(): head_row = lax.all_gather(tower_head, 'group', axis=1, tiled=True)  27.3 us
    dot_general x1, matrix products, shards(): jnp.einsum('sjcd,jhd->sjch', arrived, weight, preferred_element_type=jnp....  20.6 us
    dot_general x1, matrix products, shards(): jnp.einsum('sjch,jh->sjc', hidden, head_row.astype(jnp.float32), precisio...  14.7 us
    all_to_all x1, waiting for transfers between devices, shards(): lax.all_to_all(outgoing, 'peer', split_axis=0, concat_axis=0, tiled=True)  9.23 us
    all_to_all x1, blocking collectives, shards(): lax.all_to_all(logits, 'peer', split_axis=0, concat_axis=0, tiled=True)  6.38 us
  transfers between devices with their start and end apart: 2, of which 2 were waited for; matrix products, arithmetic and copies ran while one was open for 3% of the time, Pallas kernels for 0%

commit v1 on v0

--- a/solution.py
+++ b/solution.py
@@ -28,7 +28,24 @@
     arrived = lax.all_to_all(outgoing, "peer", split_axis=0, concat_axis=0, tiled=True)
     weight = lax.all_gather(tower_in, "group", axis=1, tiled=True)
     hidden_unit_bias = lax.all_gather(tower_bias, "group", axis=1, tiled=True)
-    head_row = lax.all_gather(tower_head, "group", axis=1, tiled=True)
+
+    def _serve_scales(xin):
+        axis_name = "group"
+        dev_n = lax.psum(1, axis_name)
+        crops = [(nth, (nth + 1) % dev_n) for nth in range(dev_n)]
+
+        def supply_kinds(y2):
+            if len(y2) == dev_n:
+                return y2
+            return supply_kinds([lax.ppermute(y2[0], axis_name, crops), *y2])
+
+        return jnp.roll(
+            jnp.concatenate(supply_kinds([xin]), axis=1),
+            shift=(lax.axis_index(axis_name) + 1) * xin.shape[1],
+            axis=1,
+        )
+
+    head_row = _serve_scales(tower_head)
     preact = jnp.einsum("sjcd,jhd->sjch", arrived, weight, preferred_element_type=jnp.float32)
     hidden = jnp.maximum(preact + hidden_unit_bias.astype(jnp.float32)[None, :, None, :], 0.0)
     logits = jnp.einsum(

time: 291 us -> 291 us (level)
  blocking collectives: 63.1 us -> 33.7 us
  waiting for transfers between devices: 163 us -> 189 us
  starting transfers between devices: 5.26 us -> 8.54 us
    ppermute x0 -> x7, waiting for transfers between devices: none -> 37.4 us  [supply_kinds(): return supply_kinds([lax.ppermute(y2[0], axis_name, crops), *y2])]
    all_gather x1 -> x0, blocking collectives: 27.3 us -> none  [shards(): head_row = lax.all_gather(tower_head, 'group', axis=1, tiled=True)]
    all_to_all x1, waiting for transfers between devices: 9.23 us -> 0.01 us  [shards(): lax.all_to_all(outgoing, 'peer', split_axis=0, concat_axis=0, tiled=True)]
    ppermute x0 -> x7, starting transfers between devices: none -> 3.28 us  [supply_kinds(): return supply_kinds([lax.ppermute(y2[0], axis_name, crops), *y2])]
  transfers between devices with their start and end apart: 2 -> 9, of which waited for: 2 -> 7; matrix products, arithmetic and copies ran while one was open for 3% -> 3% of each run, Pallas kernels for 0% -> 0%
where the time goes in v1:
time: 291 us
  waiting for transfers between devices  189 us (65%)
  matrix products  42 us (14%)
  blocking collectives  33.7 us (12%)
  between operations  13.5 us (5%)
  starting transfers between devices  8.54 us (3%)
  other arithmetic  3.12 us (1%)
    all_gather x1, waiting for transfers between devices, shards(): weight = lax.all_gather(tower_in, 'group', axis=1, tiled=True)  151 us
    ppermute x7, waiting for transfers between devices, supply_kinds(): return supply_kinds([lax.ppermute(y2[0], axis_name, crops), *y2])  37.4 us
    all_gather x1, blocking collectives, shards(): hidden_unit_bias = lax.all_gather(tower_bias, 'group', axis=1, tiled=True)  27.4 us
    dot_general x1, matrix products, shards(): jnp.einsum('sjcd,jhd->sjch', arrived, weight, preferred_element_type=jnp....  20.6 us
    dot_general x1, matrix products, shards(): jnp.einsum('sjch,jh->sjc', hidden, head_row.astype(jnp.float32), precisio...  14.7 us
    all_to_all x1, blocking collectives, shards(): lax.all_to_all(logits, 'peer', split_axis=0, concat_axis=0, tiled=True)  6.39 us
  transfers between devices with their start and end apart: 9, of which 7 were waited for; matrix products, arithmetic and copies ran while one was open for 3% of the time, Pallas kernels for 0%

profile of v1, /device:TPU:0, one launch (start us, length us, event | category | flops | bytes accessed | tf_op | source)
XLA Modules:
  0.0 290.9 jit_solution(1731920376847634211)
XLA Ops:
  6.5 0.0 copy-start
  6.5 0.0 all-gather.2.cloned.1.call-start
  6.5 0.7 all-gather.2.cloned.1.call-update
  7.3 0.7 shift-right-arithmetic_and_fusion.1
  7.9 0.9 reduce-window.6
  8.8 0.2 slice_reduce_fusion
  9.1 0.7 fusion.23
  9.8 0.8 bitcast_subtract_fusion
  10.5 0.0 copy-done
  10.5 5.0 %fusion.14 = bf16[16,176,1024]{2,1,0:T(8,128)(2,1)} fusion(s32[16,384]{1,0:T(8,128)S(1)} %bitcast_subtract_fusion, pred[16,384]{1,0:T(8,128)(4,1)S(1)} %fusion.23, bf16[384,1024]{1,0:T(8,128)(2,1)S(1)} %copy-done), kind=kOutput, calls=%fused_computation.13 | convolution fusion | flops 2219638784 | bytes 6584320 | tf_op jit(solution)/shard_map/yra,az->yrz/dot_general | solution.py:21
  15.5 0.0 copy-start.1
  15.5 0.0 copy-start.2
  15.5 5.3 %all-to-all-start = ((bf16[4,4,176,1024]{3,2,1,0:T(8,128)(2,1)}), bf16[4,4,176,1024]{3,2,1,0:T(8,128)(2,1)}, u32[]{:S(2)}, u32[]{:S(2)}) async-start(bf16[4,4,176,1024]{3,2,1,0:T(8,128)(2,1)} %bitcast.33), calls=%async_computation | async-start | bytes 11534336 | tf_op jit(solution)/shard_map/all_to_all | solution.py:28
  20.8 0.0 copy-done.1
  20.8 3.3 %collective-permute-start = (bf16[4,256]{1,0:T(4,128)(2,1)S(1)}, bf16[4,256]{1,0:T(4,128)(2,1)S(1)}, u32[]{:S(2)}, u32[]{:S(2)}) collective-permute-start(bf16[4,256]{1,0:T(4,128)(2,1)S(1)} %copy-done.1), channel_id=1, source_target_pairs={{0,4},{4,8},{8,12},{12,16},{16,20},{20,24},{24,28},{28,0},{1,5},{5... | collective-permute-start | bytes 6152 | tf_op jit(solution)/shard_map/ppermute | solution.py:40
  24.1 4.7 %collective-permute-done = bf16[4,256]{1,0:T(4,128)(2,1)S(1)} collective-permute-done((bf16[4,256]{1,0:T(4,128)(2,1)S(1)}, bf16[4,256]{1,0:T(4,128)(2,1)S(1)}, u32[]{:S(2)}, u32[]{:S(2)}) %collective-permute-start) | collective-permute-done | bytes 2080 | tf_op jit(solution)/shard_map/ppermute | solution.py:40
  28.8 0.0 collective-permute-start.1
  28.8 6.5 %collective-permute-done.1 = bf16[4,256]{1,0:T(4,128)(2,1)S(1)} collective-permute-done((bf16[4,256]{1,0:T(4,128)(2,1)S(1)}, bf16[4,256]{1,0:T(4,128)(2,1)S(1)}, u32[]{:S(2)}, u32[]{:S(2)}) %collective-permute-start.1) | collective-permute-done | bytes 2080 | tf_op jit(solution)/shard_map/ppermute | solution.py:40
  35.3 0.0 collective-permute-start.2
  35.3 6.4 %collective-permute-done.2 = bf16[4,256]{1,0:T(4,128)(2,1)S(1)} collective-permute-done((bf16[4,256]{1,0:T(4,128)(2,1)S(1)}, bf16[4,256]{1,0:T(4,128)(2,1)S(1)}, u32[]{:S(2)}, u32[]{:S(2)}) %collective-permute-start.2) | collective-permute-done | bytes 2080 | tf_op jit(solution)/shard_map/ppermute | solution.py:40
  41.7 0.0 collective-permute-start.3
  41.7 6.5 %collective-permute-done.3 = bf16[4,256]{1,0:T(4,128)(2,1)S(1)} collective-permute-done((bf16[4,256]{1,0:T(4,128)(2,1)S(1)}, bf16[4,256]{1,0:T(4,128)(2,1)S(1)}, u32[]{:S(2)}, u32[]{:S(2)}) %collective-permute-start.3) | collective-permute-done | bytes 2080 | tf_op jit(solution)/shard_map/ppermute | solution.py:40
  48.3 0.0 collective-permute-start.4
  48.3 6.6 %collective-permute-done.4 = bf16[4,256]{1,0:T(4,128)(2,1)S(1)} collective-permute-done((bf16[4,256]{1,0:T(4,128)(2,1)S(1)}, bf16[4,256]{1,0:T(4,128)(2,1)S(1)}, u32[]{:S(2)}, u32[]{:S(2)}) %collective-permute-start.4) | collective-permute-done | bytes 2080 | tf_op jit(solution)/shard_map/ppermute | solution.py:40
  54.9 0.0 collective-permute-start.5
  54.9 6.6 %collective-permute-done.5 = bf16[4,256]{1,0:T(4,128)(2,1)S(1)} collective-permute-done((bf16[4,256]{1,0:T(4,128)(2,1)S(1)}, bf16[4,256]{1,0:T(4,128)(2,1)S(1)}, u32[]{:S(2)}, u32[]{:S(2)}) %collective-permute-start.5) | collective-permute-done | bytes 2080 | tf_op jit(solution)/shard_map/ppermute | solution.py:40
  61.5 0.0 collective-permute-start.6
  61.5 0.0 copy-done.2
  61.5 27.4 %all_gather.7 = bf16[4,2048]{1,0:T(4,128)(2,1)S(1)} all-gather(bf16[4,256]{1,0:T(4,128)(2,1)S(1)} %copy-done.2), channel_id=1, replica_groups=mesh['group'=8,'peer'=4] {'group'}, dimensions={1}, use_global_device_ids=true | all-gather | bytes 18432 | tf_op jit(solution)/shard_map/all_gather | solution.py:30
  88.9 0.0 collective-permute-done.6
  89.1 0.0 all-to-all-done
  89.1 150.8 %all-gather.2.cloned.1.call-done = bf16[4,2048,1024]{2,1,0:T(8,128)(2,1)} async-done(((bf16[4,256,1024]{2,1,0:T(8,128)(2,1)}), bf16[4,2048,1024]{2,1,0:T(8,128)(2,1)}) %all-gather.2.cloned.1.call-update) | async-done | bytes 16777232 | tf_op jit(solution)/shard_map/all_gather | solution.py:29
  239.9 20.6 %fusion.4 = f32[4,4,176,2048]{3,2,1,0:T(8,128)} fusion(bf16[4,2048,1024]{2,1,0:T(8,128)(2,1)} %all-gather.2.cloned.1.call-done, bf16[4,4,176,1024]{3,2,1,0:T(8,128)(2,1)} %all-to-all-done), kind=kOutput, calls=%fused_computation.4 | convolution fusion | flops 11811160064 | bytes 45613056 | tf_op jit(solution)/shard_map/sjcd,jhd->sjch/dot_general | solution.py:49
  260.5 0.0 copy-start.3
  260.5 14.7 %fusion = f32[4,1,4,176]{3,1,2,0:T(1,128)S(1)} fusion(f32[4,4,176,2048]{3,2,1,0:T(8,128)} %fusion.4, f32[4,2048]{1,0:T(4,128)S(1)} %convert_element_type.10, bf16[4,2048,1,1]{1,0,2,3:T(4,128)(2,1)S(1)} %dynamic-slice_bitcast_fusion), kind=kOutput, calls=%fused_computation | convolution fusion | flops 80740352 | bytes 23129088 | tf_op jit(solution)/shard_map/sjch,jh->sjc/dot_general | solution.py:51
  275.2 0.0 copy-done.3
  275.2 0.1 fusion.24
  275.3 6.4 %all_to_all.10 = f32[4,4,176]{2,1,0:T(4,128)S(1)} all-to-all(f32[4,4,176]{2,1,0:T(4,128)S(1)} %fusion.24), channel_id=1, replica_groups=mesh['group'=8,'peer'=4] {'peer'}, dimensions={0} | all-to-all | bytes 22528 | tf_op jit(solution)/shard_map/all_to_all | solution.py:55
  281.7 1.8 fusion.10
  283.5 0.6 copy.22
  (20 shorter events, 0.3 us)
Async XLA Ops:
  6.5 4.0 %copy-start = (bf16[384,1024]{1,0:T(8,128)(2,1)S(1)}, bf16[384,1024]{1,0:T(8,128)(2,1)}, u32[]{:S(2)}) copy-start(bf16[384,1024]{1,0:T(8,128)(2,1)} %param.6) | copy-start | bytes 2359300
  6.5 233.4 %all-gather.2.cloned.1.call-start = ((), (), s32[]{:S(2)}) async-start(), calls=%async_computation.2 | async-start | bytes 18874368 | tf_op jit(solution)/shard_map/all_gather | solution.py:29
  15.5 5.3 %copy-start.1 = (bf16[4,256]{1,0:T(4,128)(2,1)S(1)}, bf16[4,256]{1,0:T(4,128)(2,1)}, u32[]{:S(2)}) copy-start(bf16[4,256]{1,0:T(4,128)(2,1)} %param.10) | copy-start | bytes 6148
  15.5 46.0 %copy-start.2 = (bf16[4,256]{1,0:T(4,128)(2,1)S(1)}, bf16[4,256]{1,0:T(4,128)(2,1)}, u32[]{:S(2)}) copy-start(bf16[4,256]{1,0:T(4,128)(2,1)} %param.9) | copy-start | bytes 6148
  15.5 73.6 %all-to-all-start = ((bf16[4,4,176,1024]{3,2,1,0:T(8,128)(2,1)}), bf16[4,4,176,1024]{3,2,1,0:T(8,128)(2,1)}, u32[]{:S(2)}, u32[]{:S(2)}) async-start(bf16[4,4,176,1024]{3,2,1,0:T(8,128)(2,1)} %bitcast.33), calls=%async_computation | async-start | bytes 11534336 | tf_op jit(solution)/shard_map/all_to_all | solution.py:28
  20.8 8.0 %collective-permute-start = (bf16[4,256]{1,0:T(4,128)(2,1)S(1)}, bf16[4,256]{1,0:T(4,128)(2,1)S(1)}, u32[]{:S(2)}, u32[]{:S(2)}) collective-permute-start(bf16[4,256]{1,0:T(4,128)(2,1)S(1)} %copy-done.1), channel_id=1, source_target_pairs={{0,4},{4,8},{8,12},{12,16},{16,20},{20,24},{24,28},{28,0},{1,5},{5... | collective-permute-start | bytes 6152 | tf_op jit(solution)/shard_map/ppermute | solution.py:40
  28.8 6.5 %collective-permute-start.1 = (bf16[4,256]{1,0:T(4,128)(2,1)S(1)}, bf16[4,256]{1,0:T(4,128)(2,1)S(1)}, u32[]{:S(2)}, u32[]{:S(2)}) collective-permute-start(bf16[4,256]{1,0:T(4,128)(2,1)S(1)} %collective-permute-done), channel_id=1, source_target_pairs={{0,4},{4,8},{8,12},{12,16},{16,20},{20,24},{24,28},{28,0},{1,5},{5... | collective-permute-start | bytes 6152 | tf_op jit(solution)/shard_map/ppermute | solution.py:40
  35.3 6.5 %collective-permute-start.2 = (bf16[4,256]{1,0:T(4,128)(2,1)S(1)}, bf16[4,256]{1,0:T(4,128)(2,1)S(1)}, u32[]{:S(2)}, u32[]{:S(2)}) collective-permute-start(bf16[4,256]{1,0:T(4,128)(2,1)S(1)} %collective-permute-done.1), channel_id=1, source_target_pairs={{0,4},{4,8},{8,12},{12,16},{16,20},{20,24},{24,28},{28,0},{1,5},{5... | collective-permute-start | bytes 6152 | tf_op jit(solution)/shard_map/ppermute | solution.py:40
  41.7 6.5 %collective-permute-start.3 = (bf16[4,256]{1,0:T(4,128)(2,1)S(1)}, bf16[4,256]{1,0:T(4,128)(2,1)S(1)}, u32[]{:S(2)}, u32[]{:S(2)}) collective-permute-start(bf16[4,256]{1,0:T(4,128)(2,1)S(1)} %collective-permute-done.2), channel_id=1, source_target_pairs={{0,4},{4,8},{8,12},{12,16},{16,20},{20,24},{24,28},{28,0},{1,5},{5... | collective-permute-start | bytes 6152 | tf_op jit(solution)/shard_map/ppermute | solution.py:40
  48.3 6.6 %collective-permute-start.4 = (bf16[4,256]{1,0:T(4,128)(2,1)S(1)}, bf16[4,256]{1,0:T(4,128)(2,1)S(1)}, u32[]{:S(2)}, u32[]{:S(2)}) collective-permute-start(bf16[4,256]{1,0:T(4,128)(2,1)S(1)} %collective-permute-done.3), channel_id=1, source_target_pairs={{0,4},{4,8},{8,12},{12,16},{16,20},{20,24},{24,28},{28,0},{1,5},{5... | collective-permute-start | bytes 6152 | tf_op jit(solution)/shard_map/ppermute | solution.py:40
  54.9 6.6 %collective-permute-start.5 = (bf16[4,256]{1,0:T(4,128)(2,1)S(1)}, bf16[4,256]{1,0:T(4,128)(2,1)S(1)}, u32[]{:S(2)}, u32[]{:S(2)}) collective-permute-start(bf16[4,256]{1,0:T(4,128)(2,1)S(1)} %collective-permute-done.4), channel_id=1, source_target_pairs={{0,4},{4,8},{8,12},{12,16},{16,20},{20,24},{24,28},{28,0},{1,5},{5... | collective-permute-start | bytes 6152 | tf_op jit(solution)/shard_map/ppermute | solution.py:40
  61.5 27.4 %collective-permute-start.6 = (bf16[4,256]{1,0:T(4,128)(2,1)S(1)}, bf16[4,256]{1,0:T(4,128)(2,1)S(1)}, u32[]{:S(2)}, u32[]{:S(2)}) collective-permute-start(bf16[4,256]{1,0:T(4,128)(2,1)S(1)} %collective-permute-done.5), channel_id=1, source_target_pairs={{0,4},{4,8},{8,12},{12,16},{16,20},{20,24},{24,28},{28,0},{1,5},{5... | collective-permute-start | bytes 6152 | tf_op jit(solution)/shard_map/ppermute | solution.py:40
  260.5 14.7 %copy-start.3 = (f32[4]{0:T(128)S(1)}, f32[4]{0:T(128)}, u32[]{:S(2)}) copy-start(f32[4]{0:T(128)} %param.11) | copy-start | bytes 52
Sparse Core Ops, SparseCore 0:
  9.5 230.3 all-gather.1
